TPU v7x, 512 devices: a 4x2x32 block of a 4x8x32 slice. The times are simulated.
512 devices in a mesh: groups: 2 (over y), grid: 32 (over z), row: 2 (over core), rep: 4 (over x).
Axes of the slice: x: 4, y: 2, z: 32, core: 2. Of those that a mesh axis runs over, the one named last changes fastest.
The devices are a block of a 4x8x32 slice.
Arguments:
- tokens: bfloat16 [2048, 4096], P(('groups', 'grid', 'rep'), 'row'), parts along dimension 0, may hold values from -40 to 40
- target_tokens: int32 [2048], P('groups'), parts along dimension 0, may hold values from 0 to 31999
- gate_weight: bfloat16 [4096, 14336], P(('row', 'rep'), 'grid'), may hold values from -0.09375 to 0.09375
- up_weight: bfloat16 [4096, 14336], P(('row', 'rep'), 'grid'), may hold values from -0.09375 to 0.09375
- down_weight: bfloat16 [14336, 4096], P('grid', ('row', 'rep')), may hold values from -0.046875 to 0.046875
- norm_gain: float32 [4096], P('row'), may hold values from 0.5 to 1.5
- vocab_weight: bfloat16 [4096, 32000], P('row', ('grid', 'rep')), may hold values from -6 to 6
Outputs:
- mixed: bfloat16 [2048, 4096], P(('groups', 'grid', 'rep'), 'row'), parts along dimension 0
- logprob: float32 [2048], P(('groups', 'grid', 'rep')), parts along dimension 0
There are 2 independent parts, one for each index of `groups`. A program takes and returns all parts, laid end to end along the dimension named above; an argument that names none is the same for every part. Nothing has to cross between parts.
All inputs are finite; a program needn't handle non-finite values.
Results may differ from a plain program's by a relative error of at most 0.0046.
Values may be sent and summed in bfloat16 or wider, within the bound.
No kernel may reach another device: no remote copies, remote signals or barrier semaphores. Data moves between devices by JAX's collectives and lax.ppermute only.
A program may use at most 64 MiB of HBM per device.

v0:
```python
import jax
import jax.numpy as jnp
from jax import lax
from jax.sharding import PartitionSpec as P

GATE_UP_REACH = 0.09375
DOWN_REACH = 0.046875


def parity_groups(size):
    return [list(range(side, size, 2)) for side in (0, 1)]


def swapped_in_pairs(value, axis):
    size = lax.axis_size(axis)
    return lax.ppermute(value, axis, [(i, i ^ 1) for i in range(size)])


def sent_to_all(value, axis):
    peers = lax.axis_size(axis)
    return lax.all_to_all(
        jnp.broadcast_to(value[None], (peers, *value.shape)), axis, 0, 0, tiled=True
    )


def shifted(value, axis, step):
    size = lax.axis_size(axis)
    return lax.ppermute(value, axis, [(i, (i + step) % size) for i in range(size)])


def class_groups(size):
    return [list(range(side, size, 4)) for side in range(4)]


def turned(blocks, place, sign):
    size = len(blocks)
    return [
        lax.select_n(place, *(blocks[(k + sign * j) % size] for j in range(size))) for k in range(size)
    ]


def both_halves(part, axis):
    return part + lax.ppermute(part, axis, [(0, 1), (1, 0)])


def summed_products(parts, weights):
    return sum(
        lax.dot_general(p, w, (((1,), (1,)), ((), ())), preferred_element_type=jnp.float32)
        for p, w in zip(parts, weights)
    )


def row_stats(normed, weights, targets, column_start):
    part = jnp.einsum("tk,rkv->rtv", normed, weights, preferred_element_type=jnp.float32)
    logits = both_halves(part, "row")
    ids = lax.broadcasted_iota(jnp.int32, logits.shape, 0) * logits.shape[2] + lax.broadcasted_iota(
        jnp.int32, logits.shape, 2
    )
    top = jnp.max(logits, axis=(0, 2))
    total = jnp.sum(jnp.exp(logits - top[None, :, None]), axis=(0, 2))
    picked = jnp.sum(
        jnp.where(ids == (targets - column_start)[None, :, None], logits, 0.0), axis=(0, 2)
    )
    return jnp.stack([top, total, picked])


def device_step(tokens, target_tokens, gate_weight, up_weight, down_weight, norm_gain, vocab_weight):
    own_rows, half_width = tokens.shape
    features = half_width * lax.axis_size("row")
    grid = lax.axis_size("grid")
    rep = lax.axis_size("rep")
    side = lax.rem(lax.axis_index("grid"), 2)

    units = down_weight.shape[0]
    block = jnp.concatenate([gate_weight.T, down_weight, up_weight.T], axis=0)
    after = shifted(block, "rep", -1)
    before = shifted(block, "rep", 1)

    own = lax.all_gather(tokens, "grid", axis=0, axis_index_groups=parity_groups(grid))
    own = own.reshape(-1, half_width)
    own, after, before = lax.optimization_barrier((own, after, before))
    middle = block.shape[0] // 2
    far_first = shifted(after[:middle], "rep", -1)
    far_last = shifted(before[middle:], "rep", 1)
    other = swapped_in_pairs(own, "grid")
    vocab = sent_to_all(vocab_weight, "rep")
    here = lax.axis_index("grid")
    rep_place = lax.axis_index("rep")
    quad = lax.rem(here, 4)
    second = lax.div(quad, 2)

    def by_class(rows, first):
        even, odd = (
            rows.reshape(grid // 4, 2, own_rows, half_width)[:, side].reshape(-1, half_width)
            for side in (0, 1)
        )
        return jnp.where(first == 0, even, odd), jnp.where(first == 0, odd, even)

    on_0, on_2 = by_class(own, second)
    on_1, on_3 = by_class(other, lax.rem(second + side, 2))
    sets = [turned(jnp.split(rows, rep, axis=1), rep_place, 1) for rows in (on_1, on_3, on_2, on_0)]
    parts = [jnp.concatenate(pieces, axis=0) for pieces in zip(*sets)]
    length = lax.psum(sum(jnp.sum(jnp.abs(p.astype(jnp.float32)), axis=1) for p in parts), "row")
    reach = jnp.square(GATE_UP_REACH * length) * (DOWN_REACH * units * grid)
    reach = jnp.maximum(reach, 1e-20) / 30000.0
    share = (1.0 / reach)[:, None]
    count = on_0.shape[0]

    gate_part = summed_products(
        parts, [block[:units], after[:units], far_first[:units], before[:units]]
    )
    up_part = summed_products(
        parts,
        [block[2 * units :], after[2 * units :], far_last[2 * units - middle :], before[2 * units :]],
    )
    gate_value, up_value = both_halves(gate_part, "row"), both_halves(up_part, "row")
    hidden = (jax.nn.silu(gate_value) * up_value).astype(jnp.bfloat16)
    far_down = jnp.concatenate([far_first[units:], far_last[: 2 * units - middle]], axis=0)
    downs = [block[units : 2 * units], after[units : 2 * units], far_down, before[units : 2 * units]]
    branch = [jnp.dot(hidden, w, preferred_element_type=jnp.float32) for w in downs]
    to_1, to_3, to_2, kept = (
        jnp.concatenate(turned([p[rows] for p in branch], rep_place, -1), axis=1) * share[rows]
        for rows in (slice(k * count, (k + 1) * count) for k in range(4))
    )
    from_2 = shifted(to_2.astype(jnp.float16), "grid", 2)
    from_3 = shifted(to_1.astype(jnp.float16), "grid", 1)
    from_1 = shifted(to_3.astype(jnp.float16), "grid", -1)
    pair_sum = kept + from_1.astype(jnp.float32) + from_3.astype(jnp.float32)
    pair_sum = (pair_sum + from_2.astype(jnp.float32)).astype(jnp.float16)
    branch = lax.psum(pair_sum, "grid", axis_index_groups=class_groups(grid))
    mixed_own = (
        on_0.astype(jnp.float32) + branch.astype(jnp.float32) * reach[3 * count :, None]
    ).astype(jnp.bfloat16)
    mixed = lax.dynamic_slice_in_dim(mixed_own, lax.div(here, 4) * own_rows, own_rows, 0)
    held = lax.optimization_barrier(mixed_own).astype(jnp.float32)
    squares = lax.psum(jnp.sum(held * held, axis=1), "row")
    scale = lax.rsqrt(squares / features + 1e-05)
    normed = (held * scale[:, None] * norm_gain[None, :]).astype(jnp.bfloat16)
    normed_2 = shifted(normed, "grid", 2)
    normed_3 = shifted(normed, "grid", 1)
    normed_1 = shifted(normed, "grid", -1)
    others = jnp.concatenate([normed_1, normed_2, normed_3], axis=0)

    targets = lax.dynamic_slice_in_dim(
        target_tokens.reshape(grid // 4, 4, rep, own_rows), rep_place, 1, 2
    )[:, :, 0]
    targets = turned([targets[:, k].reshape(-1) for k in range(4)], quad, 1)
    column_start = here * (vocab.shape[0] * vocab.shape[2])
    stats_own = row_stats(normed, vocab, targets[0], column_start)
    stats_others = row_stats(others, vocab, jnp.concatenate(targets[1:]), column_start)
    stats = [stats_own, *jnp.split(stats_others, 3, axis=1)]
    pieces = jnp.stack([p.reshape(3, grid // 4, own_rows) for p in turned(stats, quad, -1)])
    pieces = pieces.transpose(2, 0, 1, 3).reshape(grid, 3 * own_rows)
    found = lax.all_to_all(pieces, "grid", 0, 0, tiled=True).reshape(grid, 3, own_rows)
    top = jnp.max(found[:, 0], axis=0)
    total = jnp.sum(found[:, 1] * jnp.exp(found[:, 0] - top[None]), axis=0)
    logprob = jnp.sum(found[:, 2], axis=0) - top - jnp.log(total)
    return (mixed, logprob)


def solution(mesh):
    in_specs = (
        P(("groups", "grid", "rep"), "row"),
        P("groups"),
        P(("row", "rep"), "grid"),
        P(("row", "rep"), "grid"),
        P("grid", ("row", "rep")),
        P("row"),
        P("row", ("grid", "rep")),
    )
    out_specs = (P(("groups", "grid", "rep"), "row"), P(("groups", "grid", "rep")))
    return jax.shard_map(device_step, mesh=mesh, in_specs=in_specs, out_specs=out_specs, check_vma=False)
```

profile of v0, /device:TPU:33, one launch (start us, length us, event | category | flops | bytes accessed | tf_op | source)
XLA Modules:
  0.0 303.4 jit_solution(2473259741547549285)
XLA Ops:
  0.6 1.5 pad_maximum_fusion
  2.1 5.6 %collective-permute-start = (bf16[1344,512]{1,0:T(8,128)(2,1)S(1)}, bf16[1344,512]{1,0:T(8,128)(2,1)S(1)}, u32[]{:S(2)}, u32[]{:S(2)}) collective-permute-start(bf16[1344,512]{1,0:T(8,128)(2,1)S(1)} %pad_maximum_fusion), channel_id=1, source_target_pairs={{0,3},{1,0},{2,1},{3,2},{4,7},{5,4},{6,5},{7,6},{8,11},{9,8},{10,9... | collective-permute-start | bytes 4128776 | tf_op jit(solution)/shard_map/ppermute | solution.py:28
  7.8 2.0 collective-permute-start.1
  9.7 2.2 broadcast_in_dim.8
  12.0 5.1 %all-to-all-start = ((bf16[4,2048,250]{2,1,0:T(8,128)(2,1)}), bf16[4,2048,250]{2,1,0:T(8,128)(2,1)}, u32[]{:S(2)}, u32[]{:S(2)}) async-start(bf16[4,2048,250]{2,1,0:T(8,128)(2,1)} %broadcast_in_dim.8), calls=%async_computation | async-start | bytes 8388608 | tf_op jit(solution)/shard_map/all_to_all | solution.py:21
  17.1 70.8 %all-gather = bf16[128,2048]{1,0:T(8,128)(2,1)S(1)} all-gather(bf16[8,2048]{1,0:T(8,128)(2,1)S(1)} %copy-done.6), channel_id=2, replica_groups={{0,16,32,48,64,80,96,112,128,144,160,176,192,208,224,240},{8,24,40,56,7..., dimensions={0}, use_global_device_ids=true | all-gather | bytes 557056 | tf_op jit(solution)/shard_map/all_gather | solution.py:79
  88.0 3.8 %collective-permute-start.2 = (bf16[128,2048]{1,0:T(8,128)(2,1)S(1)}, bf16[128,2048]{1,0:T(8,128)(2,1)S(1)}, u32[]{:S(2)}, u32[]{:S(2)}) collective-permute-start(bf16[128,2048]{1,0:T(8,128)(2,1)S(1)} %all-gather), channel_id=1, source_target_pairs={{0,8},{8,0},{16,24},{24,16},{32,40},{40,32},{48,56},{56,48},{64,72... | collective-permute-start | bytes 1572872 | tf_op jit(solution)/shard_map/ppermute | solution.py:16
  91.8 1.1 slice.146
  93.0 2.0 collective-permute-start.5
  95.0 4.6 %collective-permute-start.3 = (bf16[672,512]{1,0:T(8,128)(2,1)S(1)}, bf16[672,512]{1,0:T(8,128)(2,1)S(1)}, u32[]{:S(2)}, u32[]{:S(2)}) collective-permute-start(bf16[672,512]{1,0:T(8,128)(2,1)S(1)} %slice.142), channel_id=1, source_target_pairs={{0,3},{1,0},{2,1},{3,2},{4,7},{5,4},{6,5},{7,6},{8,11},{9,8},{10,9... | collective-permute-start | bytes 2064392 | tf_op jit(solution)/shard_map/ppermute | solution.py:28
  99.9 0.8 copy-done.4
  100.7 0.3 fusion.38
  101.0 0.2 abs_reduce_fusion.2
  101.2 0.3 convolution_add_fusion.1
  101.5 1.3 fusion.26
  102.9 0.2 abs_reduce_fusion
  103.0 1.3 fusion.29
  104.4 0.3 fusion.39
  104.7 0.3 convolution_add_fusion.3
  105.0 4.1 %collective-permute-done.5 = bf16[672,512]{1,0:T(8,128)(2,1)S(1)} collective-permute-done((bf16[672,512]{1,0:T(8,128)(2,1)S(1)}, bf16[672,512]{1,0:T(8,128)(2,1)S(1)}, u32[]{:S(2)}, u32[]{:S(2)}) %collective-permute-start.5) | collective-permute-done | bytes 688160 | tf_op jit(solution)/shard_map/ppermute | solution.py:28
  109.1 0.3 fusion
  109.4 8.2 %collective-permute-start.6 = (f32[256,448]{0,1:T(8,128)S(1)}, f32[256,448]{0,1:T(8,128)}, u32[]{:S(2)}, u32[]{:S(2)}) collective-permute-start(f32[256,448]{0,1:T(8,128)S(1)} %fusion), channel_id=1, source_target_pairs={{0,4},{4,0},{1,5},{5,1},{2,6},{6,2},{3,7},{7,3},{8,12},{12,8},{9,1... | collective-permute-start | bytes 1376264 | tf_op jit(solution)/shard_map/ppermute | solution.py:43
  117.7 0.3 fusion.1
  118.0 0.6 copy-done.3
  118.6 1.9 collective-permute-start.4
  120.5 2.7 psum.21
  123.3 1.3 multiply_convert_fusion
  124.6 0.3 fusion.22
  125.0 1.4 fusion.24
  126.4 0.3 fusion.43
  126.7 0.3 fusion.18
  127.7 2.0 collective-permute-start.9
  129.7 2.0 collective-permute-start.8
  131.8 32.8 %collective-permute-start.7 = (f16[64,2048]{1,0:T(8,128)(2,1)S(1)}, f16[64,2048]{1,0:T(8,128)(2,1)S(1)}, u32[]{:S(2)}, u32[]{:S(2)}) collective-permute-start(f16[64,2048]{1,0:T(8,128)(2,1)S(1)} %fusion.13), channel_id=1, source_target_pairs={{0,248},{8,0},{16,8},{24,16},{32,24},{40,32},{48,40},{56,48},{64,5... | collective-permute-start | bytes 786440 | tf_op jit(solution)/shard_map/ppermute | solution.py:28
  164.7 0.1 reshape.138
  164.9 1.7 collective-permute-done.9
  166.6 11.6 %collective-permute-done.8 = f16[64,2048]{1,0:T(8,128)(2,1)S(1)} collective-permute-done((f16[64,2048]{1,0:T(8,128)(2,1)S(1)}, f16[64,2048]{1,0:T(8,128)(2,1)S(1)}, u32[]{:S(2)}, u32[]{:S(2)}) %collective-permute-start.8) | collective-permute-done | bytes 262176 | tf_op jit(solution)/shard_map/ppermute | solution.py:28
  178.1 0.2 fusion.12
  178.3 42.8 %all-reduce.1 = u32[4,16384]{1,0:T(4,128)S(1)} all-reduce(u32[4,16384]{1,0:T(4,128)S(1)} %bitcast.91), channel_id=1, replica_groups={{0,32,64,96,128,160,192,224},{8,40,72,104,136,168,200,232},{16,48,80,11..., use_global_device_ids=true, to_apply=%region_5.6.clone | all-reduce | flops 65536 | bytes 524288 | tf_op jit(solution)/shard_map/psum | solution.py:130
  221.2 0.1 add_convert_fusion
  221.3 0.2 fusion.6
  221.5 9.7 %psum.23 = f32[64]{0:T(128)S(1)} all-reduce(f32[64]{0:T(128)S(1)} %fusion.6), channel_id=1, replica_groups=mesh['groups'=2,'grid'=32,'row'=2,'rep'=4] {'row'}, use_global_device_ids=true, to_apply=%region_7.8 | all-reduce | flops 64 | bytes 512 | tf_op jit(solution)/shard_map/psum | solution.py:136
  231.2 0.1 fusion.8
  231.3 3.4 %collective-permute-start.13 = (bf16[64,2048]{1,0:T(8,128)(2,1)S(1)}, bf16[64,2048]{1,0:T(8,128)(2,1)S(1)}, u32[]{:S(2)}, u32[]{:S(2)}) collective-permute-start(bf16[64,2048]{1,0:T(8,128)(2,1)S(1)} %fusion.8), channel_id=1, source_target_pairs={{0,8},{8,16},{16,24},{24,32},{32,40},{40,48},{48,56},{56,64},{64,7... | collective-permute-start | bytes 786440 | tf_op jit(solution)/shard_map/ppermute | solution.py:28
  234.8 3.2 %collective-permute-start.12 = (bf16[64,2048]{1,0:T(8,128)(2,1)S(1)}, bf16[64,2048]{1,0:T(8,128)(2,1)S(1)}, u32[]{:S(2)}, u32[]{:S(2)}) collective-permute-start(bf16[64,2048]{1,0:T(8,128)(2,1)S(1)} %fusion.8), channel_id=1, source_target_pairs={{0,16},{8,24},{16,32},{24,40},{32,48},{40,56},{48,64},{56,72},{64,... | collective-permute-start | bytes 786440 | tf_op jit(solution)/shard_map/ppermute | solution.py:28
  238.0 4.6 %collective-permute-start.11 = (bf16[64,2048]{1,0:T(8,128)(2,1)S(1)}, bf16[64,2048]{1,0:T(8,128)(2,1)S(1)}, u32[]{:S(2)}, u32[]{:S(2)}) collective-permute-start(bf16[64,2048]{1,0:T(8,128)(2,1)S(1)} %fusion.8), channel_id=1, source_target_pairs={{0,248},{8,0},{16,8},{24,16},{32,24},{40,32},{48,40},{56,48},{64,5... | collective-permute-start | bytes 786440 | tf_op jit(solution)/shard_map/ppermute | solution.py:28
  242.6 1.3 collective-permute-done.13
  243.9 4.7 %collective-permute-done.12 = bf16[64,2048]{1,0:T(8,128)(2,1)S(1)} collective-permute-done((bf16[64,2048]{1,0:T(8,128)(2,1)S(1)}, bf16[64,2048]{1,0:T(8,128)(2,1)S(1)}, u32[]{:S(2)}, u32[]{:S(2)}) %collective-permute-start.12) | collective-permute-done | bytes 262176 | tf_op jit(solution)/shard_map/ppermute | solution.py:28
  248.6 3.2 %convolution_bitcast_fusion = f32[4,192,250]{2,1,0:T(8,128)S(1)} fusion(bf16[4,2048,250]{2,1,0:T(8,128)(2,1)} %all-to-all-done, bf16[64,2048]{1,0:T(8,128)(2,1)S(1)} %collective-permute-done.13, bf16[64,2048]{1,0:T(8,128)(2,1)S(1)} %collective-permute-done.12, bf16[64,2048]{1,0:T(8,128)(2,1)S(1)} %collective-permute-done.11), kind=kOutput, calls=%fused_computation.1 | convolution fusion | flops 788791296 | bytes 5650432 | tf_op jit(solution)/shard_map/tk,rkv->rtv/dot_general | solution.py:54
  251.8 3.3 %collective-permute-start.14 = (f32[4,192,250]{2,1,0:T(8,128)S(1)}, f32[4,192,250]{2,1,0:T(8,128)S(1)}, u32[]{:S(2)}, u32[]{:S(2)}) collective-permute-start(f32[4,192,250]{2,1,0:T(8,128)S(1)} %convolution_bitcast_fusion), channel_id=1, source_target_pairs={{0,4},{4,0},{1,5},{5,1},{2,6},{6,2},{3,7},{7,3},{8,12},{12,8},{9,1... | collective-permute-start | bytes 2304008 | tf_op jit(solution)/shard_map/ppermute | solution.py:43
  255.0 3.0 convolution_bitcast_fusion.1
  258.0 2.0 collective-permute-start.10
  260.4 1.1 collective-permute-done.10
  261.5 0.1 fusion.40
  261.6 0.2 exponential_reduce_fusion.1
  261.9 0.2 fusion.41
  262.0 0.4 exponential_reduce_fusion
  262.9 0.7 all_to_all.10
  263.6 18.2 %all-to-all-start.1 = ((f32[32,1,24]{2,1,0:T(1,128)}), f32[32,1,24]{2,1,0:T(1,128)S(1)}, u32[]{:S(2)}, u32[]{:S(2)}) async-start(f32[32,1,24]{2,1,0:T(1,128)} %bitcast.20), calls=%async_computation.1 | async-start | bytes 32768 | tf_op jit(solution)/shard_map/all_to_all | solution.py:154
  281.8 0.6 constant_dynamic-slice_fusion.1
  282.4 20.0 %all-to-all-done.1 = f32[32,1,24]{2,1,0:T(1,128)S(1)} async-done(((f32[32,1,24]{2,1,0:T(1,128)}), f32[32,1,24]{2,1,0:T(1,128)S(1)}, u32[]{:S(2)}, u32[]{:S(2)}) %all-to-all-start.1) | async-done | bytes 3104 | tf_op jit(solution)/shard_map/all_to_all | solution.py:154
  302.5 0.2 slice_reduce_fusion
  302.6 0.2 fusion.34
  302.8 0.5 log_subtract_fusion
  (72 shorter events, 2.3 us)
Async XLA Ops:
  0.6 9.1 %copy-start.1 = (bf16[2048,250]{1,0:T(8,128)(2,1)S(1)}, bf16[2048,250]{1,0:T(8,128)(2,1)}, u32[]{:S(2)}) copy-start(bf16[2048,250]{1,0:T(8,128)(2,1)} %param.13) | copy-start | bytes 3072004
  2.1 85.8 %collective-permute-start = (bf16[1344,512]{1,0:T(8,128)(2,1)S(1)}, bf16[1344,512]{1,0:T(8,128)(2,1)S(1)}, u32[]{:S(2)}, u32[]{:S(2)}) collective-permute-start(bf16[1344,512]{1,0:T(8,128)(2,1)S(1)} %pad_maximum_fusion), channel_id=1, source_target_pairs={{0,3},{1,0},{2,1},{3,2},{4,7},{5,4},{6,5},{7,6},{8,11},{9,8},{10,9... | collective-permute-start | bytes 4128776 | tf_op jit(solution)/shard_map/ppermute | solution.py:28
  7.8 80.2 %collective-permute-start.1 = (bf16[1344,512]{1,0:T(8,128)(2,1)S(1)}, bf16[1344,512]{1,0:T(8,128)(2,1)}, u32[]{:S(2)}, u32[]{:S(2)}) collective-permute-start(bf16[1344,512]{1,0:T(8,128)(2,1)S(1)} %pad_maximum_fusion), channel_id=1, source_target_pairs={{0,1},{1,2},{2,3},{3,0},{4,5},{5,6},{6,7},{7,4},{8,9},{9,10},{10,1... | collective-permute-start | bytes 4128776 | tf_op jit(solution)/shard_map/ppermute | solution.py:28
  12.0 5.1 %copy-start.6 = (bf16[8,2048]{1,0:T(8,128)(2,1)S(1)}, bf16[8,2048]{1,0:T(8,128)(2,1)}, u32[]{:S(2)}) copy-start(bf16[8,2048]{1,0:T(8,128)(2,1)} %param.7) | copy-start | bytes 98308
  12.0 236.6 %all-to-all-start = ((bf16[4,2048,250]{2,1,0:T(8,128)(2,1)}), bf16[4,2048,250]{2,1,0:T(8,128)(2,1)}, u32[]{:S(2)}, u32[]{:S(2)}) async-start(bf16[4,2048,250]{2,1,0:T(8,128)(2,1)} %broadcast_in_dim.8), calls=%async_computation | async-start | bytes 8388608 | tf_op jit(solution)/shard_map/all_to_all | solution.py:21
  88.0 11.8 %collective-permute-start.2 = (bf16[128,2048]{1,0:T(8,128)(2,1)S(1)}, bf16[128,2048]{1,0:T(8,128)(2,1)S(1)}, u32[]{:S(2)}, u32[]{:S(2)}) collective-permute-start(bf16[128,2048]{1,0:T(8,128)(2,1)S(1)} %all-gather), channel_id=1, source_target_pairs={{0,8},{8,0},{16,24},{24,16},{32,40},{40,32},{48,56},{56,48},{64,72... | collective-permute-start | bytes 1572872 | tf_op jit(solution)/shard_map/ppermute | solution.py:16
  93.0 16.2 %collective-permute-start.5 = (bf16[672,512]{1,0:T(8,128)(2,1)S(1)}, bf16[672,512]{1,0:T(8,128)(2,1)S(1)}, u32[]{:S(2)}, u32[]{:S(2)}) collective-permute-start(bf16[672,512]{1,0:T(8,128)(2,1)S(1)} %slice.146), channel_id=1, source_target_pairs={{0,1},{1,2},{2,3},{3,0},{4,5},{5,6},{6,7},{7,4},{8,9},{9,10},{10,1... | collective-permute-start | bytes 2064392 | tf_op jit(solution)/shard_map/ppermute | solution.py:28
  95.0 22.7 %collective-permute-start.3 = (bf16[672,512]{1,0:T(8,128)(2,1)S(1)}, bf16[672,512]{1,0:T(8,128)(2,1)S(1)}, u32[]{:S(2)}, u32[]{:S(2)}) collective-permute-start(bf16[672,512]{1,0:T(8,128)(2,1)S(1)} %slice.142), channel_id=1, source_target_pairs={{0,3},{1,0},{2,1},{3,2},{4,7},{5,4},{6,5},{7,6},{8,11},{9,8},{10,9... | collective-permute-start | bytes 2064392 | tf_op jit(solution)/shard_map/ppermute | solution.py:28
  99.7 1.0 copy-start.4
  102.8 1.5 copy-start.5
  109.1 14.2 %copy-start.2 = (bf16[672,512]{1,0:T(8,128)(2,1)}, bf16[672,512]{1,0:T(8,128)(2,1)S(1)}, u32[]{:S(2)}) copy-start(bf16[672,512]{1,0:T(8,128)(2,1)S(1)} %collective-permute-done.5) | copy-start | bytes 2064388
  109.4 13.9 %collective-permute-start.6 = (f32[256,448]{0,1:T(8,128)S(1)}, f32[256,448]{0,1:T(8,128)}, u32[]{:S(2)}, u32[]{:S(2)}) collective-permute-start(f32[256,448]{0,1:T(8,128)S(1)} %fusion), channel_id=1, source_target_pairs={{0,4},{4,0},{1,5},{5,1},{2,6},{6,2},{3,7},{7,3},{8,12},{12,8},{9,1... | collective-permute-start | bytes 1376264 | tf_op jit(solution)/shard_map/ppermute | solution.py:43
  117.7 0.9 copy-start.3
  118.6 4.7 %collective-permute-start.4 = (f32[256,448]{0,1:T(8,128)S(1)}, f32[256,448]{0,1:T(8,128)}, u32[]{:S(2)}, u32[]{:S(2)}) collective-permute-start(f32[256,448]{0,1:T(8,128)S(1)} %fusion.1), channel_id=1, source_target_pairs={{0,4},{4,0},{1,5},{5,1},{2,6},{6,2},{3,7},{7,3},{8,12},{12,8},{9,1... | collective-permute-start | bytes 1376264 | tf_op jit(solution)/shard_map/ppermute | solution.py:43
  124.6 1.8 copy-start
  125.0 1.8 slice-start
  125.0 1.8 slice-start.1
  127.5 37.1 %copy-start.8 = (s32[1024]{0:T(1024)S(1)}, s32[1024]{0:T(1024)}, u32[]{:S(2)}) copy-start(s32[1024]{0:T(1024)} %param.8) | copy-start | bytes 12292
  127.7 38.9 %collective-permute-start.9 = (f16[64,2048]{1,0:T(8,128)(2,1)S(1)}, f16[64,2048]{1,0:T(8,128)(2,1)S(1)}, u32[]{:S(2)}, u32[]{:S(2)}) collective-permute-start(f16[64,2048]{1,0:T(8,128)(2,1)S(1)} %fusion.15), channel_id=1, source_target_pairs={{0,16},{8,24},{16,32},{24,40},{32,48},{40,56},{48,64},{56,72},{64,... | collective-permute-start | bytes 786440 | tf_op jit(solution)/shard_map/ppermute | solution.py:28
  129.7 48.4 %collective-permute-start.8 = (f16[64,2048]{1,0:T(8,128)(2,1)S(1)}, f16[64,2048]{1,0:T(8,128)(2,1)S(1)}, u32[]{:S(2)}, u32[]{:S(2)}) collective-permute-start(f16[64,2048]{1,0:T(8,128)(2,1)S(1)} %fusion.14), channel_id=1, source_target_pairs={{0,8},{8,16},{16,24},{24,32},{32,40},{40,48},{48,56},{56,64},{64,7... | collective-permute-start | bytes 786440 | tf_op jit(solution)/shard_map/ppermute | solution.py:28
  131.8 46.3 %collective-permute-start.7 = (f16[64,2048]{1,0:T(8,128)(2,1)S(1)}, f16[64,2048]{1,0:T(8,128)(2,1)S(1)}, u32[]{:S(2)}, u32[]{:S(2)}) collective-permute-start(f16[64,2048]{1,0:T(8,128)(2,1)S(1)} %fusion.13), channel_id=1, source_target_pairs={{0,248},{8,0},{16,8},{24,16},{32,24},{40,32},{48,40},{56,48},{64,5... | collective-permute-start | bytes 786440 | tf_op jit(solution)/shard_map/ppermute | solution.py:28
  178.1 53.1 %copy-start.7 = (f32[2048]{0:T(1024)S(1)}, f32[2048]{0:T(1024)}, u32[]{:S(2)}) copy-start(f32[2048]{0:T(1024)} %param.12) | copy-start | bytes 24580
  231.3 12.6 %collective-permute-start.13 = (bf16[64,2048]{1,0:T(8,128)(2,1)S(1)}, bf16[64,2048]{1,0:T(8,128)(2,1)S(1)}, u32[]{:S(2)}, u32[]{:S(2)}) collective-permute-start(bf16[64,2048]{1,0:T(8,128)(2,1)S(1)} %fusion.8), channel_id=1, source_target_pairs={{0,8},{8,16},{16,24},{24,32},{32,40},{40,48},{48,56},{56,64},{64,7... | collective-permute-start | bytes 786440 | tf_op jit(solution)/shard_map/ppermute | solution.py:28
  234.8 13.8 %collective-permute-start.12 = (bf16[64,2048]{1,0:T(8,128)(2,1)S(1)}, bf16[64,2048]{1,0:T(8,128)(2,1)S(1)}, u32[]{:S(2)}, u32[]{:S(2)}) collective-permute-start(bf16[64,2048]{1,0:T(8,128)(2,1)S(1)} %fusion.8), channel_id=1, source_target_pairs={{0,16},{8,24},{16,32},{24,40},{32,48},{40,56},{48,64},{56,72},{64,... | collective-permute-start | bytes 786440 | tf_op jit(solution)/shard_map/ppermute | solution.py:28
  238.0 10.6 %collective-permute-start.11 = (bf16[64,2048]{1,0:T(8,128)(2,1)S(1)}, bf16[64,2048]{1,0:T(8,128)(2,1)S(1)}, u32[]{:S(2)}, u32[]{:S(2)}) collective-permute-start(bf16[64,2048]{1,0:T(8,128)(2,1)S(1)} %fusion.8), channel_id=1, source_target_pairs={{0,248},{8,0},{16,8},{24,16},{32,24},{40,32},{48,40},{56,48},{64,5... | collective-permute-start | bytes 786440 | tf_op jit(solution)/shard_map/ppermute | solution.py:28
  251.8 10.1 %collective-permute-start.14 = (f32[4,192,250]{2,1,0:T(8,128)S(1)}, f32[4,192,250]{2,1,0:T(8,128)S(1)}, u32[]{:S(2)}, u32[]{:S(2)}) collective-permute-start(f32[4,192,250]{2,1,0:T(8,128)S(1)} %convolution_bitcast_fusion), channel_id=1, source_target_pairs={{0,4},{4,0},{1,5},{5,1},{2,6},{6,2},{3,7},{7,3},{8,12},{12,8},{9,1... | collective-permute-start | bytes 2304008 | tf_op jit(solution)/shard_map/ppermute | solution.py:43
  258.0 3.5 %collective-permute-start.10 = (f32[4,64,250]{2,1,0:T(8,128)S(1)}, f32[4,64,250]{2,1,0:T(8,128)S(1)}, u32[]{:S(2)}, u32[]{:S(2)}) collective-permute-start(f32[4,64,250]{2,1,0:T(8,128)S(1)} %convolution_bitcast_fusion.1), channel_id=1, source_target_pairs={{0,4},{4,0},{1,5},{5,1},{2,6},{6,2},{3,7},{7,3},{8,12},{12,8},{9,1... | collective-permute-start | bytes 768008 | tf_op jit(solution)/shard_map/ppermute | solution.py:43
  263.6 38.8 %all-to-all-start.1 = ((f32[32,1,24]{2,1,0:T(1,128)}), f32[32,1,24]{2,1,0:T(1,128)S(1)}, u32[]{:S(2)}, u32[]{:S(2)}) async-start(f32[32,1,24]{2,1,0:T(1,128)} %bitcast.20), calls=%async_computation.1 | async-start | bytes 32768 | tf_op jit(solution)/shard_map/all_to_all | solution.py:154
where the time goes:
time: 304 us; the launch traced here: 303 us
  blocking collectives  126 us (41%)
  starting transfers between devices  105 us (35%)
  waiting for transfers between devices  44.4 us (15%)
  matrix products  13 us (4%)
  local copies, waits for them, and re-layouts  7.16 us (2%)
  other arithmetic  6.87 us (2%)
    all_gather x1, blocking collectives, device_step(): lax.all_gather(tokens, 'grid', axis=0, axis_index_groups=parity_groups(gr...  70.8 us
    ppermute x10, starting transfers between devices, shifted(): lax.ppermute(value, axis, [(i, (i + step) % size) for i in range(size)])  62.1 us
    psum x1, blocking collectives, device_step(): branch = lax.psum(pair_sum, 'grid', axis_index_groups=class_groups(grid))  42.8 us
    ppermute x10, waiting for transfers between devices, shifted(): lax.ppermute(value, axis, [(i, (i + step) % size) for i in range(size)])  23.3 us
    all_to_all x1, waiting for transfers between devices, device_step(): lax.all_to_all(pieces, 'grid', 0, 0, tiled=True).reshape(grid, 3, own_rows)  20 us
    all_to_all x1, starting transfers between devices, device_step(): lax.all_to_all(pieces, 'grid', 0, 0, tiled=True).reshape(grid, 3, own_rows)  18.2 us
    ppermute x4, starting transfers between devices, both_halves(): return part + lax.ppermute(part, axis, [(0, 1), (1, 0)])  15.4 us
    psum x1, blocking collectives, device_step(): squares = lax.psum(jnp.sum(held * held, axis=1), 'row')  9.72 us
  transfers between devices with their start and end apart: 17, of which 7 were waited for; matrix products, arithmetic and copies ran while one was open for 6% of the time, Pallas kernels for 0%

commit v1 on v0

--- a/solution.py
+++ b/solution.py
@@ -30,6 +30,11 @@
 
 def class_groups(size):
     return [list(range(side, size, 4)) for side in range(4)]
+
+
+def halves_both_ways(value, axis, step):
+    first, last = jnp.split(value, 2, axis=1)
+    return shifted(first, axis, step), shifted(last, axis, -step)
 
 
 def turned(blocks, place, sign):
@@ -122,11 +127,11 @@
         jnp.concatenate(turned([p[rows] for p in branch], rep_place, -1), axis=1) * share[rows]
         for rows in (slice(k * count, (k + 1) * count) for k in range(4))
     )
-    from_2 = shifted(to_2.astype(jnp.float16), "grid", 2)
+    from_2 = halves_both_ways(to_2.astype(jnp.float16), "grid", 2)
     from_3 = shifted(to_1.astype(jnp.float16), "grid", 1)
     from_1 = shifted(to_3.astype(jnp.float16), "grid", -1)
     pair_sum = kept + from_1.astype(jnp.float32) + from_3.astype(jnp.float32)
-    pair_sum = (pair_sum + from_2.astype(jnp.float32)).astype(jnp.float16)
+    pair_sum = (pair_sum + jnp.concatenate(from_2, axis=1).astype(jnp.float32)).astype(jnp.float16)
     branch = lax.psum(pair_sum, "grid", axis_index_groups=class_groups(grid))
     mixed_own = (
         on_0.astype(jnp.float32) + branch.astype(jnp.float32) * reach[3 * count :, None]
@@ -136,10 +141,10 @@
     squares = lax.psum(jnp.sum(held * held, axis=1), "row")
     scale = lax.rsqrt(squares / features + 1e-05)
     normed = (held * scale[:, None] * norm_gain[None, :]).astype(jnp.bfloat16)
-    normed_2 = shifted(normed, "grid", 2)
+    normed_2 = halves_both_ways(normed, "grid", 2)
     normed_3 = shifted(normed, "grid", 1)
     normed_1 = shifted(normed, "grid", -1)
-    others = jnp.concatenate([normed_1, normed_2, normed_3], axis=0)
+    others = jnp.concatenate([normed_1, jnp.concatenate(normed_2, axis=1), normed_3], axis=0)
 
     targets = lax.dynamic_slice_in_dim(
         target_tokens.reshape(grid // 4, 4, rep, own_rows), rep_place, 1, 2

time: 304 us -> 300 us (0.987)
  blocking collectives: 126 us -> 122 us
    ppermute x10 -> x12, starting transfers between devices: 62.1 us -> 69.1 us  [shifted(): lax.ppermute(value, axis, [(i, (i + step) % size) for i in range(size)])]
    all_to_all x1, starting transfers between devices: 18.2 us -> 11.4 us  [device_step(): lax.all_to_all(pieces, 'grid', 0, 0, tiled=True).reshape(grid, 3, own_rows)]
    psum x1, blocking collectives: 9.72 us -> 5.52 us  [device_step(): squares = lax.psum(jnp.sum(held * held, axis=1), 'row')]
    ppermute x10 -> x12, waiting for transfers between devices: 23.3 us -> 22.5 us  [shifted(): lax.ppermute(value, axis, [(i, (i + step) % size) for i in range(size)])]
  transfers between devices with their start and end apart: 17 -> 19, of which waited for: 7 -> 7; matrix products, arithmetic and copies ran while one was open for 6% -> 6% of each run, Pallas kernels for 0% -> 0%
where the time goes in v1:
time: 300 us; the launch traced here: 298 us
  blocking collectives  122 us (41%)
  starting transfers between devices  104 us (35%)
  waiting for transfers between devices  43.5 us (14%)
  matrix products  13 us (4%)
  local copies, waits for them, and re-layouts  7.18 us (2%)
  other arithmetic  6.96 us (2%)
    all_gather x1, blocking collectives, device_step(): lax.all_gather(tokens, 'grid', axis=0, axis_index_groups=parity_groups(gr...  70.8 us
    ppermute x12, starting transfers between devices, shifted(): lax.ppermute(value, axis, [(i, (i + step) % size) for i in range(size)])  69.1 us
    psum x1, blocking collectives, device_step(): branch = lax.psum(pair_sum, 'grid', axis_index_groups=class_groups(grid))  43.1 us
    ppermute x12, waiting for transfers between devices, shifted(): lax.ppermute(value, axis, [(i, (i + step) % size) for i in range(size)])  22.5 us
    all_to_all x1, waiting for transfers between devices, device_step(): lax.all_to_all(pieces, 'grid', 0, 0, tiled=True).reshape(grid, 3, own_rows)  20 us
    ppermute x4, starting transfers between devices, both_halves(): return part + lax.ppermute(part, axis, [(0, 1), (1, 0)])  14.8 us
    all_to_all x1, starting transfers between devices, device_step(): lax.all_to_all(pieces, 'grid', 0, 0, tiled=True).reshape(grid, 3, own_rows)  11.4 us
    dot_general x2, matrix products, row_stats(): jnp.einsum('tk,rkv->rtv', normed, weights, preferred_element_type=jnp.flo...  6.16 us
  transfers between devices with their start and end apart: 19, of which 7 were waited for; matrix products, arithmetic and copies ran while one was open for 6% of the time, Pallas kernels for 0%

profile of v1, /device:TPU:33, one launch (start us, length us, event | category | flops | bytes accessed | tf_op | source)
XLA Modules:
  0.0 298.4 jit_solution(12578140795634932210)
XLA Ops:
  0.6 1.5 pad_maximum_fusion
  2.1 5.6 %collective-permute-start = (bf16[1344,512]{1,0:T(8,128)(2,1)S(1)}, bf16[1344,512]{1,0:T(8,128)(2,1)S(1)}, u32[]{:S(2)}, u32[]{:S(2)}) collective-permute-start(bf16[1344,512]{1,0:T(8,128)(2,1)S(1)} %pad_maximum_fusion), channel_id=1, source_target_pairs={{0,3},{1,0},{2,1},{3,2},{4,7},{5,4},{6,5},{7,6},{8,11},{9,8},{10,9... | collective-permute-start | bytes 4128776 | tf_op jit(solution)/shard_map/ppermute | solution.py:28
  7.8 2.0 collective-permute-start.1
  9.7 2.2 broadcast_in_dim.8
  12.0 5.1 %all-to-all-start = ((bf16[4,2048,250]{2,1,0:T(8,128)(2,1)}), bf16[4,2048,250]{2,1,0:T(8,128)(2,1)}, u32[]{:S(2)}, u32[]{:S(2)}) async-start(bf16[4,2048,250]{2,1,0:T(8,128)(2,1)} %broadcast_in_dim.8), calls=%async_computation | async-start | bytes 8388608 | tf_op jit(solution)/shard_map/all_to_all | solution.py:21
  17.1 70.8 %all-gather = bf16[128,2048]{1,0:T(8,128)(2,1)S(1)} all-gather(bf16[8,2048]{1,0:T(8,128)(2,1)S(1)} %copy-done.6), channel_id=2, replica_groups={{0,16,32,48,64,80,96,112,128,144,160,176,192,208,224,240},{8,24,40,56,7..., dimensions={0}, use_global_device_ids=true | all-gather | bytes 557056 | tf_op jit(solution)/shard_map/all_gather | solution.py:84
  88.0 3.8 %collective-permute-start.2 = (bf16[128,2048]{1,0:T(8,128)(2,1)S(1)}, bf16[128,2048]{1,0:T(8,128)(2,1)S(1)}, u32[]{:S(2)}, u32[]{:S(2)}) collective-permute-start(bf16[128,2048]{1,0:T(8,128)(2,1)S(1)} %all-gather), channel_id=1, source_target_pairs={{0,8},{8,0},{16,24},{24,16},{32,40},{40,32},{48,56},{56,48},{64,72... | collective-permute-start | bytes 1572872 | tf_op jit(solution)/shard_map/ppermute | solution.py:16
  91.8 1.1 slice.146
  93.0 2.0 collective-permute-start.5
  95.0 4.6 %collective-permute-start.3 = (bf16[672,512]{1,0:T(8,128)(2,1)S(1)}, bf16[672,512]{1,0:T(8,128)(2,1)S(1)}, u32[]{:S(2)}, u32[]{:S(2)}) collective-permute-start(bf16[672,512]{1,0:T(8,128)(2,1)S(1)} %slice.142), channel_id=1, source_target_pairs={{0,3},{1,0},{2,1},{3,2},{4,7},{5,4},{6,5},{7,6},{8,11},{9,8},{10,9... | collective-permute-start | bytes 2064392 | tf_op jit(solution)/shard_map/ppermute | solution.py:28
  99.9 0.8 copy-done.4
  100.6 0.3 fusion.40
  101.0 0.2 abs_reduce_fusion.2
  101.1 0.3 convolution_add_fusion.1
  101.5 1.4 fusion.28
  102.9 0.2 abs_reduce_fusion
  103.0 1.3 fusion.31
  104.4 0.3 fusion.41
  104.7 0.3 convolution_add_fusion.3
  105.0 4.1 %collective-permute-done.5 = bf16[672,512]{1,0:T(8,128)(2,1)S(1)} collective-permute-done((bf16[672,512]{1,0:T(8,128)(2,1)S(1)}, bf16[672,512]{1,0:T(8,128)(2,1)S(1)}, u32[]{:S(2)}, u32[]{:S(2)}) %collective-permute-start.5) | collective-permute-done | bytes 688160 | tf_op jit(solution)/shard_map/ppermute | solution.py:28
  109.1 0.3 fusion
  109.4 8.2 %collective-permute-start.6 = (f32[256,448]{0,1:T(8,128)S(1)}, f32[256,448]{0,1:T(8,128)}, u32[]{:S(2)}, u32[]{:S(2)}) collective-permute-start(f32[256,448]{0,1:T(8,128)S(1)} %fusion), channel_id=1, source_target_pairs={{0,4},{4,0},{1,5},{5,1},{2,6},{6,2},{3,7},{7,3},{8,12},{12,8},{9,1... | collective-permute-start | bytes 1376264 | tf_op jit(solution)/shard_map/ppermute | solution.py:48
  117.7 0.3 fusion.1
  118.0 0.6 copy-done.3
  118.6 1.9 collective-permute-start.4
  120.5 2.7 psum.21
  123.3 1.3 multiply_convert_fusion
  124.7 0.3 fusion.24
  125.0 1.3 fusion.26
  126.3 0.3 fusion.47
  126.7 0.3 fusion.20
  127.1 0.2 select_select_fusion
  127.7 2.0 collective-permute-start.8
  129.8 32.8 %collective-permute-start.7 = (f16[64,2048]{1,0:T(8,128)(2,1)S(1)}, f16[64,2048]{1,0:T(8,128)(2,1)S(1)}, u32[]{:S(2)}, u32[]{:S(2)}) collective-permute-start(f16[64,2048]{1,0:T(8,128)(2,1)S(1)} %fusion.15), channel_id=1, source_target_pairs={{0,248},{8,0},{16,8},{24,16},{32,24},{40,32},{48,40},{56,48},{64,5... | collective-permute-start | bytes 786440 | tf_op jit(solution)/shard_map/ppermute | solution.py:28
  162.8 3.1 %collective-permute-start.10 = (f16[64,1024]{1,0:T(8,128)(2,1)S(1)}, f16[64,1024]{1,0:T(8,128)(2,1)S(1)}, u32[]{:S(2)}, u32[]{:S(2)}) collective-permute-start(f16[64,1024]{1,0:T(8,128)(2,1)S(1)} %get-tuple-element.41), channel_id=1, source_target_pairs={{0,240},{8,248},{16,0},{24,8},{32,16},{40,24},{48,32},{56,40},{64,... | collective-permute-start | bytes 393224 | tf_op jit(solution)/shard_map/ppermute | solution.py:28
  165.9 3.1 %collective-permute-start.9 = (f16[64,1024]{1,0:T(8,128)(2,1)S(1)}, f16[64,1024]{1,0:T(8,128)(2,1)S(1)}, u32[]{:S(2)}, u32[]{:S(2)}) collective-permute-start(f16[64,1024]{1,0:T(8,128)(2,1)S(1)} %get-tuple-element.40), channel_id=1, source_target_pairs={{0,16},{8,24},{16,32},{24,40},{32,48},{40,56},{48,64},{56,72},{64,... | collective-permute-start | bytes 393224 | tf_op jit(solution)/shard_map/ppermute | solution.py:28
  169.3 4.1 %collective-permute-done.10 = f16[64,1024]{1,0:T(8,128)(2,1)S(1)} collective-permute-done((f16[64,1024]{1,0:T(8,128)(2,1)S(1)}, f16[64,1024]{1,0:T(8,128)(2,1)S(1)}, u32[]{:S(2)}, u32[]{:S(2)}) %collective-permute-start.10) | collective-permute-done | bytes 131104 | tf_op jit(solution)/shard_map/ppermute | solution.py:28
  173.4 4.3 %collective-permute-done.9 = f16[64,1024]{1,0:T(8,128)(2,1)S(1)} collective-permute-done((f16[64,1024]{1,0:T(8,128)(2,1)S(1)}, f16[64,1024]{1,0:T(8,128)(2,1)S(1)}, u32[]{:S(2)}, u32[]{:S(2)}) %collective-permute-start.9) | collective-permute-done | bytes 131104 | tf_op jit(solution)/shard_map/ppermute | solution.py:28
  177.7 0.2 fusion.14
  177.9 43.1 %all-reduce.1 = u32[4,16384]{1,0:T(4,128)S(1)} all-reduce(u32[4,16384]{1,0:T(4,128)S(1)} %bitcast.91), channel_id=1, replica_groups={{0,32,64,96,128,160,192,224},{8,40,72,104,136,168,200,232},{16,48,80,11..., use_global_device_ids=true, to_apply=%region_5.6.clone | all-reduce | flops 65536 | bytes 524288 | tf_op jit(solution)/shard_map/psum | solution.py:135
  221.0 0.1 add_convert_fusion
  221.2 0.2 fusion.8
  221.3 5.5 %psum.23 = f32[64]{0:T(128)S(1)} all-reduce(f32[64]{0:T(128)S(1)} %fusion.8), channel_id=1, replica_groups=mesh['groups'=2,'grid'=32,'row'=2,'rep'=4] {'row'}, use_global_device_ids=true, to_apply=%region_7.8 | all-reduce | flops 64 | bytes 512 | tf_op jit(solution)/shard_map/psum | solution.py:141
  227.0 3.4 %collective-permute-start.15 = (bf16[64,2048]{1,0:T(8,128)(2,1)S(1)}, bf16[64,2048]{1,0:T(8,128)(2,1)S(1)}, u32[]{:S(2)}, u32[]{:S(2)}) collective-permute-start(bf16[64,2048]{1,0:T(8,128)(2,1)S(1)} %fusion.10), channel_id=1, source_target_pairs={{0,8},{8,16},{16,24},{24,32},{32,40},{40,48},{48,56},{56,64},{64,7... | collective-permute-start | bytes 786440 | tf_op jit(solution)/shard_map/ppermute | solution.py:28
  230.4 3.2 %collective-permute-start.12 = (bf16[64,2048]{1,0:T(8,128)(2,1)S(1)}, bf16[64,2048]{1,0:T(8,128)(2,1)S(1)}, u32[]{:S(2)}, u32[]{:S(2)}) collective-permute-start(bf16[64,2048]{1,0:T(8,128)(2,1)S(1)} %fusion.10), channel_id=1, source_target_pairs={{0,248},{8,0},{16,8},{24,16},{32,24},{40,32},{48,40},{56,48},{64,5... | collective-permute-start | bytes 786440 | tf_op jit(solution)/shard_map/ppermute | solution.py:28
  233.6 5.4 %collective-permute-start.14 = (bf16[64,1024]{1,0:T(8,128)(2,1)S(1)}, bf16[64,1024]{1,0:T(8,128)(2,1)S(1)}, u32[]{:S(2)}, u32[]{:S(2)}) collective-permute-start(bf16[64,1024]{1,0:T(8,128)(2,1)S(1)} %get-tuple-element.39), channel_id=1, source_target_pairs={{0,240},{8,248},{16,0},{24,8},{32,16},{40,24},{48,32},{56,40},{64,... | collective-permute-start | bytes 393224 | tf_op jit(solution)/shard_map/ppermute | solution.py:28
  239.0 2.0 collective-permute-start.13
  241.0 2.5 collective-permute-done.14
  243.6 7.5 %collective-permute-done.13 = bf16[64,1024]{1,0:T(8,128)(2,1)S(1)} collective-permute-done((bf16[64,1024]{1,0:T(8,128)(2,1)S(1)}, bf16[64,1024]{1,0:T(8,128)(2,1)S(1)}, u32[]{:S(2)}, u32[]{:S(2)}) %collective-permute-start.13) | collective-permute-done | bytes 131104 | tf_op jit(solution)/shard_map/ppermute | solution.py:28
  251.0 3.2 %convolution_bitcast_fusion = f32[4,192,250]{2,1,0:T(8,128)S(1)} fusion(bf16[4,2048,250]{2,1,0:T(8,128)(2,1)} %all-to-all-done, bf16[64,2048]{1,0:T(8,128)(2,1)S(1)} %collective-permute-done.15, bf16[64,1024]{1,0:T(8,128)(2,1)S(1)} %collective-permute-done.14, bf16[64,1024]{1,0:T(8,128)(2,1)S(1)} %collective-permute-done.13, ...), kind=kOutput, calls=%fused_computation.1 | convolution fusion | flops 789577728 | bytes 5650432 | tf_op jit(solution)/shard_map/tk,rkv->rtv/dot_general | solution.py:59
  254.2 2.7 collective-permute-start.16
  256.9 3.0 %convolution_bitcast_fusion.1 = f32[4,64,250]{2,1,0:T(8,128)S(1)} fusion(bf16[4,2048,250]{2,1,0:T(8,128)(2,1)} %all-to-all-done, bf16[64,2048]{1,0:T(8,128)(2,1)S(1)} %fusion.10), kind=kOutput, calls=%fused_computation.8 | convolution fusion | flops 262144000 | bytes 4614144 | tf_op jit(solution)/shard_map/tk,rkv->rtv/dot_general | solution.py:59
  259.9 2.0 collective-permute-start.11
  262.3 1.1 collective-permute-done.11
  263.5 0.2 exponential_reduce_fusion.1
  263.7 0.2 fusion.43
  263.9 0.4 exponential_reduce_fusion
  264.8 0.7 all_to_all.10
  265.5 11.4 %all-to-all-start.1 = ((f32[32,1,24]{2,1,0:T(1,128)}), f32[32,1,24]{2,1,0:T(1,128)S(1)}, u32[]{:S(2)}, u32[]{:S(2)}) async-start(f32[32,1,24]{2,1,0:T(1,128)} %bitcast.20), calls=%async_computation.1 | async-start | bytes 32768 | tf_op jit(solution)/shard_map/all_to_all | solution.py:159
  276.9 0.6 constant_dynamic-slice_fusion.1
  277.5 20.0 %all-to-all-done.1 = f32[32,1,24]{2,1,0:T(1,128)S(1)} async-done(((f32[32,1,24]{2,1,0:T(1,128)}), f32[32,1,24]{2,1,0:T(1,128)S(1)}, u32[]{:S(2)}, u32[]{:S(2)}) %all-to-all-start.1) | async-done | bytes 3104 | tf_op jit(solution)/shard_map/all_to_all | solution.py:159
  297.5 0.2 slice_reduce_fusion
  297.7 0.2 fusion.36
  297.9 0.5 log_subtract_fusion
  (78 shorter events, 2.6 us)
Async XLA Ops:
  0.6 9.1 %copy-start.1 = (bf16[2048,250]{1,0:T(8,128)(2,1)S(1)}, bf16[2048,250]{1,0:T(8,128)(2,1)}, u32[]{:S(2)}) copy-start(bf16[2048,250]{1,0:T(8,128)(2,1)} %param.13) | copy-start | bytes 3072004
  2.1 85.8 %collective-permute-start = (bf16[1344,512]{1,0:T(8,128)(2,1)S(1)}, bf16[1344,512]{1,0:T(8,128)(2,1)S(1)}, u32[]{:S(2)}, u32[]{:S(2)}) collective-permute-start(bf16[1344,512]{1,0:T(8,128)(2,1)S(1)} %pad_maximum_fusion), channel_id=1, source_target_pairs={{0,3},{1,0},{2,1},{3,2},{4,7},{5,4},{6,5},{7,6},{8,11},{9,8},{10,9... | collective-permute-start | bytes 4128776 | tf_op jit(solution)/shard_map/ppermute | solution.py:28
  7.8 80.2 %collective-permute-start.1 = (bf16[1344,512]{1,0:T(8,128)(2,1)S(1)}, bf16[1344,512]{1,0:T(8,128)(2,1)}, u32[]{:S(2)}, u32[]{:S(2)}) collective-permute-start(bf16[1344,512]{1,0:T(8,128)(2,1)S(1)} %pad_maximum_fusion), channel_id=1, source_target_pairs={{0,1},{1,2},{2,3},{3,0},{4,5},{5,6},{6,7},{7,4},{8,9},{9,10},{10,1... | collective-permute-start | bytes 4128776 | tf_op jit(solution)/shard_map/ppermute | solution.py:28
  12.0 5.1 %copy-start.6 = (bf16[8,2048]{1,0:T(8,128)(2,1)S(1)}, bf16[8,2048]{1,0:T(8,128)(2,1)}, u32[]{:S(2)}) copy-start(bf16[8,2048]{1,0:T(8,128)(2,1)} %param.7) | copy-start | bytes 98308
  12.0 239.1 %all-to-all-start = ((bf16[4,2048,250]{2,1,0:T(8,128)(2,1)}), bf16[4,2048,250]{2,1,0:T(8,128)(2,1)}, u32[]{:S(2)}, u32[]{:S(2)}) async-start(bf16[4,2048,250]{2,1,0:T(8,128)(2,1)} %broadcast_in_dim.8), calls=%async_computation | async-start | bytes 8388608 | tf_op jit(solution)/shard_map/all_to_all | solution.py:21
  88.0 11.8 %collective-permute-start.2 = (bf16[128,2048]{1,0:T(8,128)(2,1)S(1)}, bf16[128,2048]{1,0:T(8,128)(2,1)S(1)}, u32[]{:S(2)}, u32[]{:S(2)}) collective-permute-start(bf16[128,2048]{1,0:T(8,128)(2,1)S(1)} %all-gather), channel_id=1, source_target_pairs={{0,8},{8,0},{16,24},{24,16},{32,40},{40,32},{48,56},{56,48},{64,72... | collective-permute-start | bytes 1572872 | tf_op jit(solution)/shard_map/ppermute | solution.py:16
  93.0 16.2 %collective-permute-start.5 = (bf16[672,512]{1,0:T(8,128)(2,1)S(1)}, bf16[672,512]{1,0:T(8,128)(2,1)S(1)}, u32[]{:S(2)}, u32[]{:S(2)}) collective-permute-start(bf16[672,512]{1,0:T(8,128)(2,1)S(1)} %slice.146), channel_id=1, source_target_pairs={{0,1},{1,2},{2,3},{3,0},{4,5},{5,6},{6,7},{7,4},{8,9},{9,10},{10,1... | collective-permute-start | bytes 2064392 | tf_op jit(solution)/shard_map/ppermute | solution.py:28
  95.0 22.7 %collective-permute-start.3 = (bf16[672,512]{1,0:T(8,128)(2,1)S(1)}, bf16[672,512]{1,0:T(8,128)(2,1)S(1)}, u32[]{:S(2)}, u32[]{:S(2)}) collective-permute-start(bf16[672,512]{1,0:T(8,128)(2,1)S(1)} %slice.142), channel_id=1, source_target_pairs={{0,3},{1,0},{2,1},{3,2},{4,7},{5,4},{6,5},{7,6},{8,11},{9,8},{10,9... | collective-permute-start | bytes 2064392 | tf_op jit(solution)/shard_map/ppermute | solution.py:28
  99.6 1.0 copy-start.4
  101.5 2.9 copy-start.5
  109.1 14.2 %copy-start.2 = (bf16[672,512]{1,0:T(8,128)(2,1)}, bf16[672,512]{1,0:T(8,128)(2,1)S(1)}, u32[]{:S(2)}) copy-start(bf16[672,512]{1,0:T(8,128)(2,1)S(1)} %collective-permute-done.5) | copy-start | bytes 2064388
  109.4 13.9 %collective-permute-start.6 = (f32[256,448]{0,1:T(8,128)S(1)}, f32[256,448]{0,1:T(8,128)}, u32[]{:S(2)}, u32[]{:S(2)}) collective-permute-start(f32[256,448]{0,1:T(8,128)S(1)} %fusion), channel_id=1, source_target_pairs={{0,4},{4,0},{1,5},{5,1},{2,6},{6,2},{3,7},{7,3},{8,12},{12,8},{9,1... | collective-permute-start | bytes 1376264 | tf_op jit(solution)/shard_map/ppermute | solution.py:48
  117.7 0.9 copy-start.3
  118.6 4.7 %collective-permute-start.4 = (f32[256,448]{0,1:T(8,128)S(1)}, f32[256,448]{0,1:T(8,128)}, u32[]{:S(2)}, u32[]{:S(2)}) collective-permute-start(f32[256,448]{0,1:T(8,128)S(1)} %fusion.1), channel_id=1, source_target_pairs={{0,4},{4,0},{1,5},{5,1},{2,6},{6,2},{3,7},{7,3},{8,12},{12,8},{9,1... | collective-permute-start | bytes 1376264 | tf_op jit(solution)/shard_map/ppermute | solution.py:48
  124.6 1.7 copy-start
  124.6 2.0 slice-start
  124.6 2.0 slice-start.1
  127.6 41.5 %copy-start.8 = (s32[1024]{0:T(1024)S(1)}, s32[1024]{0:T(1024)}, u32[]{:S(2)}) copy-start(s32[1024]{0:T(1024)} %param.8) | copy-start | bytes 12292
  127.7 50.0 %collective-permute-start.8 = (f16[64,2048]{1,0:T(8,128)(2,1)S(1)}, f16[64,2048]{1,0:T(8,128)(2,1)S(1)}, u32[]{:S(2)}, u32[]{:S(2)}) collective-permute-start(f16[64,2048]{1,0:T(8,128)(2,1)S(1)} %fusion.16), channel_id=1, source_target_pairs={{0,8},{8,16},{16,24},{24,32},{32,40},{40,48},{48,56},{56,64},{64,7... | collective-permute-start | bytes 786440 | tf_op jit(solution)/shard_map/ppermute | solution.py:28
  129.8 47.9 %collective-permute-start.7 = (f16[64,2048]{1,0:T(8,128)(2,1)S(1)}, f16[64,2048]{1,0:T(8,128)(2,1)S(1)}, u32[]{:S(2)}, u32[]{:S(2)}) collective-permute-start(f16[64,2048]{1,0:T(8,128)(2,1)S(1)} %fusion.15), channel_id=1, source_target_pairs={{0,248},{8,0},{16,8},{24,16},{32,24},{40,32},{48,40},{56,48},{64,5... | collective-permute-start | bytes 786440 | tf_op jit(solution)/shard_map/ppermute | solution.py:28
  162.8 10.6 %collective-permute-start.10 = (f16[64,1024]{1,0:T(8,128)(2,1)S(1)}, f16[64,1024]{1,0:T(8,128)(2,1)S(1)}, u32[]{:S(2)}, u32[]{:S(2)}) collective-permute-start(f16[64,1024]{1,0:T(8,128)(2,1)S(1)} %get-tuple-element.41), channel_id=1, source_target_pairs={{0,240},{8,248},{16,0},{24,8},{32,16},{40,24},{48,32},{56,40},{64,... | collective-permute-start | bytes 393224 | tf_op jit(solution)/shard_map/ppermute | solution.py:28
  165.9 11.7 %collective-permute-start.9 = (f16[64,1024]{1,0:T(8,128)(2,1)S(1)}, f16[64,1024]{1,0:T(8,128)(2,1)S(1)}, u32[]{:S(2)}, u32[]{:S(2)}) collective-permute-start(f16[64,1024]{1,0:T(8,128)(2,1)S(1)} %get-tuple-element.40), channel_id=1, source_target_pairs={{0,16},{8,24},{16,32},{24,40},{32,48},{40,56},{48,64},{56,72},{64,... | collective-permute-start | bytes 393224 | tf_op jit(solution)/shard_map/ppermute | solution.py:28
  177.7 49.2 %copy-start.7 = (f32[2048]{0:T(1024)S(1)}, f32[2048]{0:T(1024)}, u32[]{:S(2)}) copy-start(f32[2048]{0:T(1024)} %param.12) | copy-start | bytes 24580
  227.0 24.0 %collective-permute-start.15 = (bf16[64,2048]{1,0:T(8,128)(2,1)S(1)}, bf16[64,2048]{1,0:T(8,128)(2,1)S(1)}, u32[]{:S(2)}, u32[]{:S(2)}) collective-permute-start(bf16[64,2048]{1,0:T(8,128)(2,1)S(1)} %fusion.10), channel_id=1, source_target_pairs={{0,8},{8,16},{16,24},{24,32},{32,40},{40,48},{48,56},{56,64},{64,7... | collective-permute-start | bytes 786440 | tf_op jit(solution)/shard_map/ppermute | solution.py:28
  230.4 20.7 %collective-permute-start.12 = (bf16[64,2048]{1,0:T(8,128)(2,1)S(1)}, bf16[64,2048]{1,0:T(8,128)(2,1)S(1)}, u32[]{:S(2)}, u32[]{:S(2)}) collective-permute-start(bf16[64,2048]{1,0:T(8,128)(2,1)S(1)} %fusion.10), channel_id=1, source_target_pairs={{0,248},{8,0},{16,8},{24,16},{32,24},{40,32},{48,40},{56,48},{64,5... | collective-permute-start | bytes 786440 | tf_op jit(solution)/shard_map/ppermute | solution.py:28
  233.6 10.0 %collective-permute-start.14 = (bf16[64,1024]{1,0:T(8,128)(2,1)S(1)}, bf16[64,1024]{1,0:T(8,128)(2,1)S(1)}, u32[]{:S(2)}, u32[]{:S(2)}) collective-permute-start(bf16[64,1024]{1,0:T(8,128)(2,1)S(1)} %get-tuple-element.39), channel_id=1, source_target_pairs={{0,240},{8,248},{16,0},{24,8},{32,16},{40,24},{48,32},{56,40},{64,... | collective-permute-start | bytes 393224 | tf_op jit(solution)/shard_map/ppermute | solution.py:28
  239.0 12.0 %collective-permute-start.13 = (bf16[64,1024]{1,0:T(8,128)(2,1)S(1)}, bf16[64,1024]{1,0:T(8,128)(2,1)S(1)}, u32[]{:S(2)}, u32[]{:S(2)}) collective-permute-start(bf16[64,1024]{1,0:T(8,128)(2,1)S(1)} %get-tuple-element.38), channel_id=1, source_target_pairs={{0,16},{8,24},{16,32},{24,40},{32,48},{40,56},{48,64},{56,72},{64,... | collective-permute-start | bytes 393224 | tf_op jit(solution)/shard_map/ppermute | solution.py:28
  254.2 9.5 %collective-permute-start.16 = (f32[4,192,250]{2,1,0:T(8,128)S(1)}, f32[4,192,250]{2,1,0:T(8,128)S(1)}, u32[]{:S(2)}, u32[]{:S(2)}) collective-permute-start(f32[4,192,250]{2,1,0:T(8,128)S(1)} %convolution_bitcast_fusion), channel_id=1, source_target_pairs={{0,4},{4,0},{1,5},{5,1},{2,6},{6,2},{3,7},{7,3},{8,12},{12,8},{9,1... | collective-permute-start | bytes 2304008 | tf_op jit(solution)/shard_map/ppermute | solution.py:48
  259.9 3.5 %collective-permute-start.11 = (f32[4,64,250]{2,1,0:T(8,128)S(1)}, f32[4,64,250]{2,1,0:T(8,128)S(1)}, u32[]{:S(2)}, u32[]{:S(2)}) collective-permute-start(f32[4,64,250]{2,1,0:T(8,128)S(1)} %convolution_bitcast_fusion.1), channel_id=1, source_target_pairs={{0,4},{4,0},{1,5},{5,1},{2,6},{6,2},{3,7},{7,3},{8,12},{12,8},{9,1... | collective-permute-start | bytes 768008 | tf_op jit(solution)/shard_map/ppermute | solution.py:48
  265.5 32.0 %all-to-all-start.1 = ((f32[32,1,24]{2,1,0:T(1,128)}), f32[32,1,24]{2,1,0:T(1,128)S(1)}, u32[]{:S(2)}, u32[]{:S(2)}) async-start(f32[32,1,24]{2,1,0:T(1,128)} %bitcast.20), calls=%async_computation.1 | async-start | bytes 32768 | tf_op jit(solution)/shard_map/all_to_all | solution.py:159
